TPU v7x, 32 devices: a whole 2x2x4 slice. The times are simulated.
32 devices in a mesh: groups: 2 (over y), bank: 4 (over x, core), tensor: 4 (over z).
Axes of the slice: x: 2, y: 2, z: 4, core: 2. Of those that a mesh axis runs over, the one named last changes fastest.
Arguments:
- latest_activations: bfloat16 [64, 8192], P(('groups', 'bank'), 'tensor'), parts along dimension 0, may hold values from -6 to 6
- layer_normalizer_gains_table: bfloat16 [8192], replicated, may hold values from 0.5 to 1.5
- asker_projection: bfloat16 [8192, 8192], P('bank', 'tensor'), may hold values from -0.0625 to 0.0625
- memory_projection_stack: bfloat16 [2, 8192, 1024], P(None, 'bank', 'tensor'), may hold values from -0.0625 to 0.0625
- narrowing_factors: bfloat16 [128, 48, 8192], P('bank', None, 'tensor'), may hold values from -0.0625 to 0.0625
- widening_factors_asker: bfloat16 [128, 16, 8192], P('bank', None, 'tensor'), may hold values from -1.5 to 1.5
- widening_factors_memory: bfloat16 [128, 2, 16, 1024], P('bank', None, None, 'tensor'), may hold values from -1.5 to 1.5
- tweak_for_stream: int32 [64], P(('groups', 'bank')), parts along dimension 0, may hold values from 0 to 127
- stream_offsets: int32 [64], P(('groups', 'bank')), parts along dimension 0, may hold values from 2 to 1024
- saved_rotated_addresses: bfloat16 [64, 1024, 8, 128], P(('groups', 'bank'), None, 'tensor'), parts along dimension 0, may hold values from -1200 to 1200
- saved_contents: bfloat16 [64, 1024, 8, 128], P(('groups', 'bank'), None, 'tensor'), parts along dimension 0, may hold values from -6 to 6
Outputs:
- attention: bfloat16 [64, 8192], P(('groups', 'bank'), 'tensor'), parts along dimension 0
There are 2 independent parts, one for each index of `groups`. A program takes and returns all parts, laid end to end along the dimension named above; an argument that names none is the same for every part. Nothing has to cross between parts.
All inputs are finite; a program needn't handle non-finite values.
Results may differ from a plain program's by a relative error of at most 0.0095.
The roundings to bfloat16 on the way count: a program that leaves them out, or rounds other values in their place, can miss the bound.
Values may be sent and summed in bfloat16 or wider, within the bound.
No kernel may reach another device: no remote copies, remote signals or barrier semaphores. Data moves between devices by JAX's collectives and lax.ppermute only.
A program may use at most 64 MiB of HBM per device.

v0:
```python
import math
import jax
import jax.numpy as jnp
from jax import lax
from jax.sharding import PartitionSpec as P

rope_base = 500000.0
tweak_strength = 2.0
epsilon = 1e-05


def rotate(values, positions):
    half_dim = values.shape[-1] // 2
    freqs = rope_base ** (-(jnp.arange(half_dim, dtype=jnp.float32) * 2.0) / values.shape[-1])
    angles = positions.astype(jnp.float32)[:, None] * freqs[None, :]
    cosine = jnp.cos(angles)[:, None, :]
    sine_part = jnp.sin(angles)[:, None, :]
    front_half = values[..., :half_dim]
    back_half = values[..., half_dim:]
    return jnp.concatenate(
        [front_half * cosine - back_half * sine_part, back_half * cosine + front_half * sine_part],
        axis=-1,
    )


def attend_local(
    probe_vectors, current_lookup_vectors, values_new, cache_keys, cache_values, stream_offsets
):
    reciprocal_sqrt_dim = 1.0 / math.sqrt(probe_vectors.shape[-1])
    scores = (
        jnp.einsum("bkgd,bpkd->bkgp", probe_vectors, cache_keys, preferred_element_type=jnp.float32)
        * reciprocal_sqrt_dim
    )
    self_logit = (
        jnp.einsum(
            "atcj,atj->atc",
            probe_vectors,
            current_lookup_vectors,
            preferred_element_type=jnp.float32,
        )
        * reciprocal_sqrt_dim
    )
    positions = lax.broadcasted_iota(jnp.int32, scores.shape, 3)
    live_mask = positions < stream_offsets[:, None, None, None]
    peak_score = jnp.maximum(jnp.max(jnp.where(live_mask, scores, -jnp.inf), axis=-1), self_logit)
    expo = jnp.where(live_mask, jnp.exp(scores - peak_score[..., None]), 0.0)
    own_expo = jnp.exp(self_logit - peak_score)
    total = jnp.sum(expo, axis=-1) + own_expo
    weights = (expo / total[..., None]).astype(jnp.bfloat16)
    own_weight = (own_expo / total).astype(jnp.bfloat16)
    mixed = jnp.einsum("bkgp,bpkd->bkgd", weights, cache_values, preferred_element_type=jnp.float32)
    return (
        mixed
        + own_weight.astype(jnp.float32)[..., None] * values_new.astype(jnp.float32)[:, :, None, :]
    )


def shards(
    latest_activations,
    layer_normalizer_gains_table,
    asker_projection,
    memory_projection_stack,
    narrowing_factors,
    widening_factors_asker,
    widening_factors_memory,
    tweak_for_stream,
    stream_offsets,
    saved_rotated_addresses,
    saved_contents,
):
    joined_rows = lax.all_gather(latest_activations, "tensor", axis=1, tiled=True)
    tok_float = joined_rows.astype(jnp.float32)
    mean_square = jnp.mean(tok_float * tok_float, axis=1, keepdims=True)
    normed = (
        tok_float
        * lax.rsqrt(mean_square + epsilon)
        * layer_normalizer_gains_table.astype(jnp.float32)[None, :]
    ).astype(jnp.bfloat16)
    n_bank = lax.axis_size("bank")
    n_tensor = lax.axis_size("tensor")
    bank_index = lax.axis_index("bank")
    tensor_index = lax.axis_index("tensor")
    model_width = normed.shape[1]
    piece_bank = model_width // n_bank
    piece_tensor = model_width // n_tensor
    row_count = latest_activations.shape[0]
    every_row, all_ids = (
        lax.all_gather(normed, "bank", axis=0, tiled=True),
        lax.all_gather(tweak_for_stream, "bank", axis=0, tiled=True),
    )
    base_input = lax.dynamic_slice_in_dim(every_row, bank_index * piece_bank, piece_bank, 1)
    hidden_after_rmsnorm = lax.dynamic_slice_in_dim(
        every_row, tensor_index * piece_tensor, piece_tensor, 1
    )
    sequences_on_device = narrowing_factors.shape[0]
    low_dim_extent = widening_factors_asker.shape[1]
    owned_ids = bank_index * sequences_on_device + jnp.arange(sequences_on_device, dtype=jnp.int32)
    picked = all_ids[None, :] == owned_ids[:, None]
    projected_low_vector = jnp.einsum(
        "omk,lk->oml", narrowing_factors, hidden_after_rmsnorm, preferred_element_type=jnp.float32
    )
    inner_part = jnp.sum(jnp.where(picked[:, None, :], projected_low_vector, 0.0), axis=0)
    inner_sum = lax.psum(inner_part, "tensor")
    inner_low = inner_sum.astype(jnp.bfloat16)
    pick_low = picked.astype(jnp.bfloat16)

    def spread(rank_block):
        expanded = pick_low[:, None, :] * rank_block[None, :, :]
        return expanded.reshape(sequences_on_device * low_dim_extent, rank_block.shape[1])

    probe_proj_span = asker_projection.shape[1]
    shared_proj_span = memory_projection_stack.shape[2]
    probe_correction = jnp.einsum(
        "cs,co->so",
        spread(inner_low[0:low_dim_extent]),
        widening_factors_asker.reshape(sequences_on_device * low_dim_extent, probe_proj_span),
        preferred_element_type=jnp.float32,
    )
    lookup_correction = jnp.einsum(
        "cs,co->so",
        spread(inner_low[low_dim_extent : 2 * low_dim_extent]),
        widening_factors_memory[:, 0].reshape(
            sequences_on_device * low_dim_extent, shared_proj_span
        ),
        preferred_element_type=jnp.float32,
    )
    payload_correction = jnp.einsum(
        "cs,co->so",
        spread(inner_low[2 * low_dim_extent : 3 * low_dim_extent]),
        widening_factors_memory[:, 1].reshape(
            sequences_on_device * low_dim_extent, shared_proj_span
        ),
        preferred_element_type=jnp.float32,
    )
    tweak_contribution = tweak_strength * jnp.concatenate(
        [probe_correction, lookup_correction, payload_correction], axis=1
    )
    untouched_share = lax.psum_scatter(
        jnp.concatenate(
            [
                jnp.dot(base_input, asker_projection, preferred_element_type=jnp.float32),
                jnp.dot(base_input, memory_projection_stack[0], preferred_element_type=jnp.float32),
                jnp.dot(base_input, memory_projection_stack[1], preferred_element_type=jnp.float32),
            ],
            axis=1,
        ),
        "bank",
        scatter_dimension=0,
        tiled=True,
    )
    accumulated_total = untouched_share + lax.psum_scatter(
        tweak_contribution, "bank", scatter_dimension=0, tiled=True
    )
    head_dim = saved_rotated_addresses.shape[3]
    kv_heads = saved_rotated_addresses.shape[2]
    q_heads = probe_proj_span // head_dim
    query_part = accumulated_total[:, 0:probe_proj_span].reshape(row_count, q_heads, head_dim)
    key_part = accumulated_total[:, probe_proj_span : probe_proj_span + shared_proj_span].reshape(
        row_count, kv_heads, head_dim
    )
    value_part = accumulated_total[
        :, probe_proj_span + shared_proj_span : probe_proj_span + 2 * shared_proj_span
    ].reshape(row_count, kv_heads, head_dim)
    q_rot = rotate(query_part, stream_offsets).astype(jnp.bfloat16)
    k_new = rotate(key_part, stream_offsets).astype(jnp.bfloat16)
    v_new = value_part.astype(jnp.bfloat16)
    probe_vectors = q_rot.reshape(row_count, kv_heads, q_heads // kv_heads, head_dim)
    mixed = attend_local(
        probe_vectors, k_new, v_new, saved_rotated_addresses, saved_contents, stream_offsets
    )
    return mixed.reshape(row_count, probe_proj_span).astype(jnp.bfloat16)


def solution(mesh):
    placed = (
        P(("groups", "bank"), "tensor"),
        P(),
        P("bank", "tensor"),
        P(None, "bank", "tensor"),
        P("bank", None, "tensor"),
        P("bank", None, "tensor"),
        P("bank", None, None, "tensor"),
        P(("groups", "bank")),
        P(("groups", "bank")),
        P(("groups", "bank"), None, "tensor", None),
        P(("groups", "bank"), None, "tensor", None),
    )
    return jax.shard_map(
        shards,
        mesh=mesh,
        in_specs=placed,
        out_specs=P(("groups", "bank"), "tensor"),
        check_vma=False,
    )
```

profile of v0, /device:TPU:0, one launch (start us, length us, event | category | flops | bytes accessed | tf_op | source)
XLA Modules:
  0.0 105.4 jit_solution(16486017365840379025)
XLA Ops:
  6.5 15.4 %all_gather.9 = bf16[8,8192]{1,0:T(8,128)(2,1)S(1)} all-gather(bf16[8,2048]{1,0:T(8,128)(2,1)} %param.11), channel_id=1, replica_groups=mesh['groups'=2,'bank'=4,'tensor'=4] {'tensor'}, dimensions={1}, use_global_device_ids=true | all-gather | bytes 163840 | tf_op jit(solution)/shard_map/all_gather | solution.py:71
  22.0 0.7 convert_element_type.58
  22.7 0.2 fusion.25
  22.9 0.1 fusion.27
  23.0 7.2 %all_gather.10 = bf16[32,8192]{1,0:T(8,128)(2,1)S(1)} all-gather(bf16[8,8192]{1,0:T(8,128)(2,1)S(1)} %fusion.27), channel_id=1, replica_groups=mesh['groups'=2,'bank'=4,'tensor'=4] {'bank'}, dimensions={0}, use_global_device_ids=true | all-gather | bytes 655360 | tf_op jit(solution)/shard_map/all_gather | solution.py:88
  30.2 1.5 %fusion.18 = f32[32,256]{1,0:T(8,128)S(1)} fusion(bf16[2,2048,256]{2,1,0:T(8,128)(2,1)} %param.14, bf16[32,8192]{1,0:T(8,128)(2,1)S(1)} %all_gather.10, s32[]{:T(128)S(6)} %select_n.17), kind=kOutput, calls=%fused_computation.12 | convolution fusion | flops 33554432 | bytes 1212420 | tf_op jit(solution)/shard_map/dot_general | solution.py:143
  31.7 1.5 %fusion.20 = f32[32,256]{1,0:T(8,128)S(1)} fusion(bf16[2,2048,256]{2,1,0:T(8,128)(2,1)} %param.14, bf16[32,8192]{1,0:T(8,128)(2,1)S(1)} %all_gather.10, s32[]{:T(128)S(6)} %select_n.17), kind=kOutput, calls=%fused_computation.14 | convolution fusion | flops 33554432 | bytes 1212420 | tf_op jit(solution)/shard_map/dot_general | solution.py:142
  33.2 4.9 %fusion.37 = f32[32,2048]{1,0:T(8,128)S(1)} fusion(bf16[2048,2048]{1,0:T(8,128)(2,1)} %param.13, bf16[32,8192]{1,0:T(8,128)(2,1)S(1)} %all_gather.10, s32[]{:T(128)S(6)} %select_n.17), kind=kOutput, calls=%fused_computation.39 | convolution fusion | flops 268435456 | bytes 8781828 | tf_op jit(solution)/shard_map/dot_general | solution.py:141
  38.2 0.6 dynamic-slice
  39.4 0.2 dynamic-update-slice
  39.7 4.3 %all-reduce = s32[32]{0:T(128)S(1)} all-reduce(s32[32]{0:T(128)S(1)} %dynamic-update-slice), channel_id=1, replica_groups=mesh['groups'=2,'bank'=4,'tensor'=4] {'bank'}, use_global_device_ids=true, to_apply=%add | all-reduce | flops 32 | bytes 256
  44.0 6.5 %fusion.8 = f32[48,32]{0,1:T(8,128)S(1)} fusion(bf16[32,48,2048]{2,1,0:T(8,128)(2,1)} %param.15, pred[32,32]{1,0:T(8,128)(4,1)S(1)} %get-tuple-element.21, bf16[32,8192]{1,0:T(8,128)(2,1)S(1)} %all_gather.10, s32[]{:T(128)S(6)} %select_n.18), kind=kOutput, calls=%fused_computation.8 | convolution fusion | flops 201423360 | bytes 6432772 | tf_op jit(solution)/shard_map/omk,lk->oml/dot_general | solution.py:99
  50.5 19.1 %psum.7 = bf16[48,32]{0,1:T(8,128)(2,1)S(1)} all-reduce(f32[48,32]{0,1:T(8,128)S(1)} %fusion.8), channel_id=1, replica_groups=mesh['groups'=2,'bank'=4,'tensor'=4] {'tensor'}, use_global_device_ids=true, to_apply=%region_3.4 | all-reduce | flops 1536 | bytes 9216 | tf_op jit(solution)/shard_map/psum | solution.py:103
  69.6 0.1 fusion.56
  69.7 0.1 copy.27
  69.9 0.1 copy.26
  70.0 0.2 fusion.58
  70.2 0.2 fusion.57
  70.4 0.5 convolution_bitcast_fusion
  70.9 0.8 maximum_add_fusion
  71.7 0.1 multiply_cosine_fusion
  71.8 18.3 %reduce-scatter.2.cloned.1.call-done = f32[8,2560]{1,0:T(8,128)} async-done(((f32[32,2560]{1,0:T(8,128)}), f32[8,2560]{1,0:T(8,128)}) %reduce-scatter.2.cloned.1.call-update) | async-done | bytes 81936 | tf_op jit(solution)/shard_map/reduce_scatter | solution.py:138
  90.2 1.0 slice_bitcast_fusion
  91.2 0.1 subtract_convert_fusion
  91.3 0.9 slice_bitcast_fusion.1
  92.3 0.1 maximum_bitcast_fusion
  92.4 3.5 %select_reduce_fusion = (f32[8,2,8]{2,1,0:T(2,128)S(1)}, f32[8,2,8,1024]{3,2,1,0:T(8,128)S(1)}) fusion(s32[8]{0:T(128)S(1)} %copy-done.2, bf16[8,1024,2,128]{3,2,1,0:T(2,128)(2,1)} %param.20, bf16[8,2,8,64]{3,2,1,0:T(8,128)(2,1)S(1)} %get-tuple-element.24, bf16[8,2,8,64]{3,2,1,0:T(8,128)(2,1)S(1)} %get-tuple-element.25), kind=kOutput, calls=%fused_computation.20 | convolution fusion | flops 34144128 | bytes 4751904 | tf_op jit(solution)/shard_map/bkgd,bpkd->bkgp/dot_general | solution.py:31
  95.9 0.2 fusion.41
  96.1 0.3 fusion.24
  96.4 0.7 fusion.44
  97.1 0.8 fusion.15
  97.9 0.6 copy.56
  (28 shorter events, 0.4 us)
Async XLA Ops:
  6.5 63.9 %copy-start = (bf16[32,16,2048]{2,1,0:T(8,128)(2,1)S(1)}, bf16[32,16,2048]{2,1,0:T(8,128)(2,1)}, u32[]{:S(2)}) copy-start(bf16[32,16,2048]{2,1,0:T(8,128)(2,1)} %param.16) | copy-start | bytes 6291460
  6.5 83.7 %reduce-scatter.2.cloned.1.call-start = ((), (), s32[]{:S(2)}) async-start(), calls=%async_computation.1 | async-start | bytes 409600 | tf_op jit(solution)/shard_map/reduce_scatter | solution.py:138
  33.2 5.0 %copy-start.5 = (u32[32]{0:T(128)S(1)}, u32[32]{0:T(128)}, u32[]{:S(2)}) copy-start(u32[32]{0:T(128)} %constant.39) | copy-start | bytes 388
  33.2 6.2 %copy-start.4 = (s32[8]{0:T(128)S(1)}, s32[8]{0:T(128)}, u32[]{:S(2)}) copy-start(s32[8]{0:T(128)} %param.18) | copy-start | bytes 100
  38.1 31.7 %copy-start.1 = (bf16[32,2,16,256]{3,2,1,0:T(8,128)(2,1)S(1)}, bf16[32,2,16,256]{3,2,1,0:T(8,128)(2,1)}, u32[]{:S(2)}) copy-start(bf16[32,2,16,256]{3,2,1,0:T(8,128)(2,1)} %param.17) | copy-start | bytes 1572868
  50.5 21.2 %copy-start.2 = (s32[8]{0:T(128)S(1)}, s32[8]{0:T(128)}, u32[]{:S(2)}) copy-start(s32[8]{0:T(128)} %param.19) | copy-start | bytes 100
  90.2 6.9 %copy-start.3 = (bf16[8,1024,2,128]{3,2,1,0:T(2,128)(2,1)S(1)}, bf16[8,1024,2,128]{3,2,1,0:T(2,128)(2,1)}, u32[]{:S(2)}) copy-start(bf16[8,1024,2,128]{3,2,1,0:T(2,128)(2,1)} %param.21) | copy-start | bytes 12582916
Sparse Core Ops, SparseCore 0:
  71.8 18.3 reduce-scatter.1
where the time goes:
time: 106 us; the launch traced here: 105 us
  blocking collectives  46 us (43%)
  matrix products  19.8 us (19%)
  waiting for transfers between devices  18.4 us (17%)
  between operations  14.2 us (13%)
  local copies, waits for them, and re-layouts  3.78 us (4%)
  other arithmetic  3.25 us (3%)
    psum x1, blocking collectives, shards(): inner_sum = lax.psum(inner_part, 'tensor')  19.1 us
    reduce_scatter x1, waiting for transfers between devices, shards(): lax.psum_scatter(jnp.concatenate([jnp.dot(base_input, asker_projection, p...  18.3 us
    all_gather x1, blocking collectives, shards(): lax.all_gather(latest_activations, 'tensor', axis=1, tiled=True)  15.4 us
    all_gather x1, blocking collectives, shards(): lax.all_gather(normed, 'bank', axis=0, tiled=True)  7.17 us
    dot_general x1, matrix products, shards(): jnp.einsum('omk,lk->oml', narrowing_factors, hidden_after_rmsnorm, prefer...  6.49 us
    dot_general x1, matrix products, shards(): jnp.dot(base_input, asker_projection, preferred_element_type=jnp.float32)  4.93 us
    unnamed x1, blocking collectives  4.26 us
    dot_general x1, matrix products, attend_local(): jnp.einsum('bkgd,bpkd->bkgp', probe_vectors, cache_keys, preferred_elemen...  3.5 us
  transfers between devices with their start and end apart: 1, of which 1 were waited for; matrix products, arithmetic and copies ran while one was open for 0% of the time, Pallas kernels for 0%

commit v1 on v0

--- a/solution.py
+++ b/solution.py
@@ -100,7 +100,11 @@
         "omk,lk->oml", narrowing_factors, hidden_after_rmsnorm, preferred_element_type=jnp.float32
     )
     inner_part = jnp.sum(jnp.where(picked[:, None, :], projected_low_vector, 0.0), axis=0)
-    inner_sum = lax.psum(inner_part, "tensor")
+    inner_sum = inner_part
+    for hop in (1, 2):
+        inner_sum = inner_sum + lax.ppermute(
+            inner_sum, "tensor", [(dev, dev ^ hop) for dev in range(4)]
+        )
     inner_low = inner_sum.astype(jnp.bfloat16)
     pick_low = picked.astype(jnp.bfloat16)
 

time: 106 us -> 95.3 us (0.90)
  blocking collectives: 46 us -> 26.8 us
  starting transfers between devices: 0.01 us -> 4.4 us
  waiting for transfers between devices: 18.4 us -> 22.4 us
  local copies, waits for them, and re-layouts: 3.78 us -> 5.04 us
    psum x1 -> x0, blocking collectives: 19.1 us -> none  [shards(): inner_sum = lax.psum(inner_part, 'tensor')]
    ppermute x0 -> x2, starting transfers between devices: none -> 4.39 us  [shards(): lax.ppermute(inner_sum, 'tensor', [(dev, dev ^ hop) for dev in range(4)])]
    ppermute x0 -> x2, waiting for transfers between devices: none -> 2.2 us  [shards(): lax.ppermute(inner_sum, 'tensor', [(dev, dev ^ hop) for dev in range(4)])]
    reduce_scatter x1, waiting for transfers between devices: 18.3 us -> 20.2 us  [shards(): lax.psum_scatter(jnp.concatenate([jnp.dot(base_input, asker_projection, p...]
    unnamed x16 -> x14, local copies, waits for them, and re-layouts: 1.5 us -> 2.77 us
    dot_general x1, matrix products: 1.51 us -> 0.28 us  [shards(): jnp.dot(base_input, memory_projection_stack[0], preferred_element_type=jn...]
  transfers between devices with their start and end apart: 1 -> 3, of which waited for: 1 -> 2; matrix products, arithmetic and copies ran while one was open for 0% -> 7% of each run, Pallas kernels for 0% -> 0%
where the time goes in v1:
time: 95.3 us; the launch traced here: 94.9 us
  blocking collectives  26.8 us (28%)
  waiting for transfers between devices  22.4 us (24%)
  matrix products  18.8 us (20%)
  between operations  14.2 us (15%)
  local copies, waits for them, and re-layouts  5.04 us (5%)
  starting transfers between devices  4.4 us (5%)
  other arithmetic  3.27 us (3%)
    reduce_scatter x1, waiting for transfers between devices, shards(): lax.psum_scatter(jnp.concatenate([jnp.dot(base_input, asker_projection, p...  20.2 us
    all_gather x1, blocking collectives, shards(): lax.all_gather(latest_activations, 'tensor', axis=1, tiled=True)  15.4 us
    all_gather x1, blocking collectives, shards(): lax.all_gather(normed, 'bank', axis=0, tiled=True)  7.17 us
    dot_general x1, matrix products, shards(): jnp.einsum('omk,lk->oml', narrowing_factors, hidden_after_rmsnorm, prefer...  6.49 us
    dot_general x1, matrix products, shards(): jnp.dot(base_input, asker_projection, preferred_element_type=jnp.float32)  5.08 us
    ppermute x2, starting transfers between devices, shards(): lax.ppermute(inner_sum, 'tensor', [(dev, dev ^ hop) for dev in range(4)])  4.39 us
    unnamed x1, blocking collectives  4.26 us
    dot_general x1, matrix products, attend_local(): jnp.einsum('bkgd,bpkd->bkgp', probe_vectors, cache_keys, preferred_elemen...  3.5 us
  transfers between devices with their start and end apart: 3, of which 2 were waited for; matrix products, arithmetic and copies ran while one was open for 7% of the time, Pallas kernels for 0%

profile of v1, /device:TPU:0, one launch (start us, length us, event | category | flops | bytes accessed | tf_op | source)
XLA Modules:
  0.0 94.9 jit_solution(10689348180470847986)
XLA Ops:
  6.5 15.4 %all_gather.9 = bf16[8,8192]{1,0:T(8,128)(2,1)S(1)} all-gather(bf16[8,2048]{1,0:T(8,128)(2,1)} %param.11), channel_id=1, replica_groups=mesh['groups'=2,'bank'=4,'tensor'=4] {'tensor'}, dimensions={1}, use_global_device_ids=true | all-gather | bytes 163840 | tf_op jit(solution)/shard_map/all_gather | solution.py:71
  22.0 0.7 convert_element_type.58
  22.7 0.2 fusion.25
  22.9 0.1 fusion.27
  23.0 7.2 %all_gather.10 = bf16[32,8192]{1,0:T(8,128)(2,1)S(1)} all-gather(bf16[8,8192]{1,0:T(8,128)(2,1)S(1)} %fusion.27), channel_id=1, replica_groups=mesh['groups'=2,'bank'=4,'tensor'=4] {'bank'}, dimensions={0}, use_global_device_ids=true | all-gather | bytes 655360 | tf_op jit(solution)/shard_map/all_gather | solution.py:88
  30.2 1.2 %dynamic-slice = u32[1]{0:T(128)} dynamic-slice(u32[32]{0:T(128)} %constant.39, u32[]{:T(128)S(6)} %add.62), dynamic_slice_sizes={1} | dynamic-slice | bytes 12
  32.1 0.9 dynamic-update-slice
  32.9 4.3 %all-reduce = s32[32]{0:T(128)S(1)} all-reduce(s32[32]{0:T(128)S(1)} %dynamic-update-slice), channel_id=1, replica_groups=mesh['groups'=2,'bank'=4,'tensor'=4] {'bank'}, use_global_device_ids=true, to_apply=%add | all-reduce | flops 32 | bytes 256
  37.3 6.5 %fusion.8 = f32[48,32]{0,1:T(8,128)S(1)} fusion(bf16[32,48,2048]{2,1,0:T(8,128)(2,1)} %param.15, pred[32,32]{1,0:T(8,128)(4,1)S(1)} %get-tuple-element.21, bf16[32,8192]{1,0:T(8,128)(2,1)S(1)} %all_gather.10, s32[]{:T(128)S(6)} %select_n.18), kind=kOutput, calls=%fused_computation.8 | convolution fusion | flops 201423360 | bytes 6432772 | tf_op jit(solution)/shard_map/omk,lk->oml/dot_general | solution.py:99
  43.8 1.9 %collective-permute-start = (f32[48,32]{0,1:T(8,128)S(1)}, f32[48,32]{0,1:T(8,128)S(1)}, u32[]{:S(2)}, u32[]{:S(2)}) collective-permute-start(f32[48,32]{0,1:T(8,128)S(1)} %fusion.8), channel_id=1, source_target_pairs={{0,1},{1,0},{2,3},{3,2},{4,5},{5,4},{6,7},{7,6},{8,9},{9,8},{10,11... | collective-permute-start | bytes 18440 | tf_op jit(solution)/shard_map/ppermute | solution.py:105
  45.7 1.5 %fusion.18 = f32[32,256]{1,0:T(8,128)S(1)} fusion(bf16[2,2048,256]{2,1,0:T(8,128)(2,1)} %param.14, bf16[32,8192]{1,0:T(8,128)(2,1)S(1)} %all_gather.10, s32[]{:T(128)S(6)} %select_n.17), kind=kOutput, calls=%fused_computation.12 | convolution fusion | flops 33554432 | bytes 1212420 | tf_op jit(solution)/shard_map/dot_general | solution.py:147
  47.2 5.1 %fusion.37 = f32[32,2048]{1,0:T(8,128)S(1)} fusion(bf16[2048,2048]{1,0:T(8,128)(2,1)} %param.13, bf16[32,8192]{1,0:T(8,128)(2,1)S(1)} %all_gather.10, s32[]{:T(128)S(6)} %select_n.17), kind=kOutput, calls=%fused_computation.39 | convolution fusion | flops 268435456 | bytes 8781828 | tf_op jit(solution)/shard_map/dot_general | solution.py:145
  52.3 0.3 fusion.20
  52.6 2.5 %collective-permute-start.1 = (f32[48,32]{0,1:T(8,128)S(1)}, f32[48,32]{0,1:T(8,128)S(1)}, u32[]{:S(2)}, u32[]{:S(2)}) collective-permute-start(f32[48,32]{0,1:T(8,128)S(1)} %add.54), channel_id=1, source_target_pairs={{0,2},{1,3},{2,0},{3,1},{4,6},{5,7},{6,4},{7,5},{8,10},{9,11},{10,... | collective-permute-start | bytes 18440 | tf_op jit(solution)/shard_map/ppermute | solution.py:105
  55.1 2.2 %collective-permute-done.1 = f32[48,32]{0,1:T(8,128)S(1)} collective-permute-done((f32[48,32]{0,1:T(8,128)S(1)}, f32[48,32]{0,1:T(8,128)S(1)}, u32[]{:S(2)}, u32[]{:S(2)}) %collective-permute-start.1) | collective-permute-done | bytes 6176 | tf_op jit(solution)/shard_map/ppermute | solution.py:105
  57.3 0.1 fusion.56
  57.4 0.1 copy.27
  57.7 0.2 fusion.58
  57.9 0.2 fusion.57
  58.1 0.5 convolution_bitcast_fusion
  58.6 0.8 maximum_add_fusion
  59.4 0.1 multiply_cosine_fusion
  59.5 20.2 %reduce-scatter.2.cloned.1.call-done = f32[8,2560]{1,0:T(8,128)} async-done(((f32[32,2560]{1,0:T(8,128)}), f32[8,2560]{1,0:T(8,128)}) %reduce-scatter.2.cloned.1.call-update) | async-done | bytes 81936 | tf_op jit(solution)/shard_map/reduce_scatter | solution.py:142
  79.7 1.0 %slice_bitcast_fusion = f32[8,16,128]{2,0,1:T(8,128)S(1)} fusion(f32[8,2560]{1,0:T(8,128)} %reduce-scatter.2.cloned.1.call-done), kind=kLoop, calls=%fused_computation.41 | loop fusion | bytes 131072 | tf_op jit(solution)/shard_map/reshape | solution.py:161
  80.7 0.1 subtract_convert_fusion
  80.8 0.9 slice_bitcast_fusion.1
  81.8 3.5 %select_reduce_fusion = (f32[8,2,8]{2,1,0:T(2,128)S(1)}, f32[8,2,8,1024]{3,2,1,0:T(8,128)S(1)}) fusion(s32[8]{0:T(128)S(1)} %copy-done.3, bf16[8,1024,2,128]{3,2,1,0:T(2,128)(2,1)} %param.20, bf16[8,2,8,64]{3,2,1,0:T(8,128)(2,1)S(1)} %get-tuple-element.24, bf16[8,2,8,64]{3,2,1,0:T(8,128)(2,1)S(1)} %get-tuple-element.25), kind=kOutput, calls=%fused_computation.20 | convolution fusion | flops 34144128 | bytes 4751904 | tf_op jit(solution)/shard_map/bkgd,bpkd->bkgp/dot_general | solution.py:31
  85.3 0.2 fusion.41
  85.6 0.3 fusion.24
  85.9 0.7 fusion.44
  86.6 0.8 fusion.15
  87.4 0.6 copy.56
  (31 shorter events, 0.6 us)
Async XLA Ops:
  6.5 51.6 %copy-start = (bf16[32,16,2048]{2,1,0:T(8,128)(2,1)S(1)}, bf16[32,16,2048]{2,1,0:T(8,128)(2,1)}, u32[]{:S(2)}) copy-start(bf16[32,16,2048]{2,1,0:T(8,128)(2,1)} %param.16) | copy-start | bytes 6291460
  6.5 73.1 %reduce-scatter.2.cloned.1.call-start = ((), (), s32[]{:S(2)}) async-start(), calls=%async_computation.1 | async-start | bytes 409600 | tf_op jit(solution)/shard_map/reduce_scatter | solution.py:142
  43.8 8.8 %collective-permute-start = (f32[48,32]{0,1:T(8,128)S(1)}, f32[48,32]{0,1:T(8,128)S(1)}, u32[]{:S(2)}, u32[]{:S(2)}) collective-permute-start(f32[48,32]{0,1:T(8,128)S(1)} %fusion.8), channel_id=1, source_target_pairs={{0,1},{1,0},{2,3},{3,2},{4,5},{5,4},{6,7},{7,6},{8,9},{9,8},{10,11... | collective-permute-start | bytes 18440 | tf_op jit(solution)/shard_map/ppermute | solution.py:105
  47.2 5.1 %copy-start.1 = (bf16[2,2048,256]{2,1,0:T(8,128)(2,1)S(1)}, bf16[2,2048,256]{2,1,0:T(8,128)(2,1)}, u32[]{:S(2)}) copy-start(bf16[2,2048,256]{2,1,0:T(8,128)(2,1)} %param.14) | copy-start | bytes 6291460
  47.2 7.9 %copy-start.2 = (bf16[32,2,16,256]{3,2,1,0:T(8,128)(2,1)S(1)}, bf16[32,2,16,256]{3,2,1,0:T(8,128)(2,1)}, u32[]{:S(2)}) copy-start(bf16[32,2,16,256]{3,2,1,0:T(8,128)(2,1)} %param.17) | copy-start | bytes 1572868
  52.3 7.1 %copy-start.3 = (s32[8]{0:T(128)S(1)}, s32[8]{0:T(128)}, u32[]{:S(2)}) copy-start(s32[8]{0:T(128)} %param.19) | copy-start | bytes 100
  52.6 4.7 %collective-permute-start.1 = (f32[48,32]{0,1:T(8,128)S(1)}, f32[48,32]{0,1:T(8,128)S(1)}, u32[]{:S(2)}, u32[]{:S(2)}) collective-permute-start(f32[48,32]{0,1:T(8,128)S(1)} %add.54), channel_id=1, source_target_pairs={{0,2},{1,3},{2,0},{3,1},{4,6},{5,7},{6,4},{7,5},{8,10},{9,11},{10,... | collective-permute-start | bytes 18440 | tf_op jit(solution)/shard_map/ppermute | solution.py:105
  79.7 6.9 %copy-start.4 = (bf16[8,1024,2,128]{3,2,1,0:T(2,128)(2,1)S(1)}, bf16[8,1024,2,128]{3,2,1,0:T(2,128)(2,1)}, u32[]{:S(2)}) copy-start(bf16[8,1024,2,128]{3,2,1,0:T(2,128)(2,1)} %param.21) | copy-start | bytes 12582916
Sparse Core Ops, SparseCore 0:
  59.5 20.1 reduce-scatter.1
